TPU v7x, 8 devices: a whole 2x2x1 slice. The times are simulated.
8 devices in a mesh: rep: 1 (over z), kv: 8 (over y, x, core).
Axes of the slice: x: 2, y: 2, z: 1, core: 2. Of those that a mesh axis runs over, the one named last changes fastest.
Arguments:
- embeds: bfloat16 [2, 512, 4096], P(None, ('rep', 'kv'))
- w_query: bfloat16 [2, 4096, 4096], replicated
- w_key: bfloat16 [2, 4096, 1024], replicated
- w_value: bfloat16 [2, 4096, 1024], replicated
- w_out: bfloat16 [2, 4096, 4096], replicated
- w_up: bfloat16 [2, 4096, 14336], replicated
- w_down: bfloat16 [2, 14336, 4096], replicated
- k_pool: bfloat16 [1536, 2, 16, 8, 128], P(('rep', 'kv'))
- v_pool: bfloat16 [1536, 2, 16, 8, 128], P(('rep', 'kv'))
- new_table: int32 [512, 2], P('rep')
- seq_lens: int32 [512], P('rep')
- mig_src: int32 [64], P('rep')
- mig_dst: int32 [64], P('rep')
Outputs:
- output 1: bfloat16 [2, 512, 4096], P(None, ('rep', 'kv'))
- output 2: bfloat16 [1536, 2, 16, 8, 128], P(('rep', 'kv'))
- output 3: bfloat16 [1536, 2, 16, 8, 128], P(('rep', 'kv'))
All inputs are finite; a program needn't handle non-finite values.
Results may differ from a plain program's by a relative error of at most 0.0168677.
Values are sent between devices in bfloat16 or wider.
A program may use at most 2.75 GiB of HBM per device.

v0:
```python
import jax
import jax.numpy as jnp
from jax import lax
from jax.sharding import PartitionSpec as P


def local_index(slot_ids, dev_idx, slots):
    local_ids = slot_ids - dev_idx * slots
    return jnp.where((local_ids >= 0) & (local_ids < slots), local_ids, slots)


def slot_owners(page_table, dev_idx, slots):
    seq_count, page_count = page_table.shape
    seg_ids = local_index(page_table, dev_idx, slots).reshape(-1)
    seq_plus = jnp.broadcast_to(jnp.arange(1, seq_count + 1)[:, None], page_table.shape).reshape(-1)
    page_plus = jnp.broadcast_to(jnp.arange(1, page_count + 1)[None, :], page_table.shape).reshape(-1)
    owner_seq = jax.ops.segment_sum(seq_plus, seg_ids, num_segments=slots + 1)[:slots] - 1
    owner_page = jax.ops.segment_sum(page_plus, seg_ids, num_segments=slots + 1)[:slots] - 1
    return owner_seq, owner_page


def local_partials(queries_all, k_layer, v_layer, owner_seq, owner_page, seq_lens, step_idx):
    seq_count = queries_all.shape[0]
    page_len = k_layer.shape[1]
    head_dim = k_layer.shape[3]
    is_owned = owner_seq >= 0
    safe_seq = jnp.maximum(owner_seq, 0)
    q_slots = jnp.take(queries_all, safe_seq, axis=0)
    scores = jnp.einsum('skgd,sikd->skgi', q_slots, k_layer, preferred_element_type=jnp.float32) * head_dim ** -0.5
    positions = owner_page[:, None] * page_len + jnp.arange(page_len)[None, :]
    limits = jnp.take(seq_lens, safe_seq) + step_idx
    valid_mask = (is_owned[:, None] & (positions <= limits[:, None]))[:, None, None, :]
    scores = jnp.where(valid_mask, scores, -1e30)
    slot_max = jnp.max(scores, axis=-1)
    prob_vals = jnp.where(valid_mask, jnp.exp(scores - slot_max[..., None]), 0.0)
    slot_sum = jnp.sum(prob_vals, axis=-1)
    slot_out = jnp.einsum('skgi,sikd->skgd', prob_vals.astype(jnp.bfloat16), v_layer, preferred_element_type=jnp.float32)
    seg_ids = jnp.where(is_owned, owner_seq, seq_count)
    seq_max = jax.ops.segment_max(slot_max, seg_ids, num_segments=seq_count + 1)[:seq_count]
    seq_max = jnp.maximum(seq_max, -1e30)
    rescale = jnp.exp(slot_max - jnp.take(seq_max, safe_seq, axis=0))
    seq_sum = jax.ops.segment_sum(slot_sum * rescale, seg_ids, num_segments=seq_count + 1)[:seq_count]
    seq_out = jax.ops.segment_sum(slot_out * rescale[..., None], seg_ids, num_segments=seq_count + 1)[:seq_count]
    return jnp.concatenate([seq_out, seq_max[..., None], seq_sum[..., None]], axis=-1)


def merge_partials(packed, group_size):
    head_dim = packed.shape[-1] - 2
    received = lax.all_to_all(packed, 'kv', 0, 0, tiled=True)
    received = received.reshape((group_size, -1) + packed.shape[1:])
    part_out = received[..., :head_dim]
    part_max = received[..., head_dim]
    part_sum = received[..., head_dim + 1]
    glob_max = jnp.max(part_max, axis=0)
    scale_w = jnp.exp(part_max - glob_max)
    total_sum = jnp.sum(scale_w * part_sum, axis=0)
    merged = jnp.sum(scale_w[..., None] * part_out, axis=0) / total_sum[..., None]
    return merged.reshape(merged.shape[0], -1).astype(jnp.bfloat16)


def decode_layer(hidden, layer_idx, step_idx, pools, owners, page_table, seq_lens, weights, dev_idx, group_size):
    w_query, w_key, w_value, w_out, w_up, w_down = weights
    k_pool, v_pool = pools
    owner_seq, owner_page = owners
    slots = k_pool.shape[0]
    page_len = k_pool.shape[2]
    kv_heads = k_pool.shape[3]
    head_dim = k_pool.shape[4]
    num_heads = w_query.shape[2] // head_dim
    queries = jnp.dot(hidden, w_query[layer_idx], preferred_element_type=jnp.float32).astype(jnp.bfloat16)
    new_keys = jnp.dot(hidden, w_key[layer_idx], preferred_element_type=jnp.float32).astype(jnp.bfloat16)
    new_vals = jnp.dot(hidden, w_value[layer_idx], preferred_element_type=jnp.float32).astype(jnp.bfloat16)
    queries_all = lax.all_gather(queries, 'kv', axis=0, tiled=True)
    kv_all = lax.all_gather(jnp.stack([new_keys, new_vals]), 'kv', axis=1, tiled=True)
    seq_count = queries_all.shape[0]
    positions = seq_lens + step_idx
    slot_ids = jnp.take_along_axis(page_table, (positions // page_len)[:, None], axis=1)[:, 0]
    local_ids = local_index(slot_ids, dev_idx, slots)
    offsets = positions % page_len
    kv_rows = kv_all.reshape(2, seq_count, kv_heads, head_dim)
    k_pool = k_pool.at[local_ids, layer_idx, offsets].set(kv_rows[0], mode='drop')
    v_pool = v_pool.at[local_ids, layer_idx, offsets].set(kv_rows[1], mode='drop')
    packed = local_partials(queries_all.reshape(seq_count, kv_heads, num_heads // kv_heads, head_dim), k_pool[:, layer_idx], v_pool[:, layer_idx], owner_seq, owner_page, seq_lens, step_idx)
    attn_out = merge_partials(packed, group_size)
    hidden = (hidden.astype(jnp.float32) + jnp.dot(attn_out, w_out[layer_idx], preferred_element_type=jnp.float32)).astype(jnp.bfloat16)
    up_proj = jnp.dot(hidden, w_up[layer_idx], preferred_element_type=jnp.float32).astype(jnp.bfloat16)
    act_vals = jax.nn.gelu(up_proj.astype(jnp.float32), approximate=True).astype(jnp.bfloat16)
    hidden = (hidden.astype(jnp.float32) + jnp.dot(act_vals, w_down[layer_idx], preferred_element_type=jnp.float32)).astype(jnp.bfloat16)
    return hidden, (k_pool, v_pool)


def decode_step(hidden, step_idx, pools, page_table, seq_lens, weights, dev_idx, group_size):
    owners = slot_owners(page_table, dev_idx, pools[0].shape[0])
    for layer_idx in range(pools[0].shape[1]):
        hidden, pools = decode_layer(hidden, layer_idx, step_idx, pools, owners, page_table, seq_lens, weights, dev_idx, group_size)
    return hidden, pools


def migrate(pools, mig_src, mig_dst, dev_idx):
    k_pool, v_pool = pools
    slots = k_pool.shape[0]
    src_local = local_index(mig_src, dev_idx, slots)
    dst_local = local_index(mig_dst, dev_idx, slots)
    k_pages = jnp.take(k_pool, src_local, axis=0, mode='fill', fill_value=0)
    v_pages = jnp.take(v_pool, src_local, axis=0, mode='fill', fill_value=0)
    k_pages, v_pages = lax.psum((k_pages, v_pages), 'kv')
    k_pool = k_pool.at[dst_local].set(k_pages, mode='drop').at[src_local].set(0, mode='drop')
    v_pool = v_pool.at[dst_local].set(v_pages, mode='drop').at[src_local].set(0, mode='drop')
    return k_pool, v_pool


def solution(mesh):
    group_size = mesh.shape['kv']
    pool_spec = P(('rep', 'kv'))
    tok_spec = P(None, ('rep', 'kv'), None)

    def device_fn(embeds, w_query, w_key, w_value, w_out, w_up, w_down, k_pool, v_pool, new_table, seq_lens, mig_src, mig_dst):
        dev_idx = lax.axis_index('kv')
        slots = k_pool.shape[0]
        weights = (w_query, w_key, w_value, w_out, w_up, w_down)
        slot_remap = jnp.arange(slots * group_size, dtype=jnp.int32).at[mig_dst].set(mig_src)
        old_table = jnp.take(slot_remap, new_table, axis=0)
        pools = (k_pool, v_pool)
        first_out, pools = decode_step(embeds[0], 0, pools, old_table, seq_lens, weights, dev_idx, group_size)
        pools = migrate(pools, mig_src, mig_dst, dev_idx)
        second_out, pools = decode_step(embeds[1], 1, pools, new_table, seq_lens, weights, dev_idx, group_size)
        return jnp.stack([first_out, second_out]), pools[0], pools[1]

    return jax.shard_map(device_fn, mesh=mesh, in_specs=(tok_spec, P(), P(), P(), P(), P(), P(), pool_spec, pool_spec, P('rep', None), P('rep'), P('rep'), P('rep')), out_specs=(tok_spec, pool_spec, pool_spec), check_vma=False)
```

profile of v0, /device:TPU:0, one launch (start us, length us, event | category | flops | bytes accessed | tf_op | source)
XLA Modules:
  0.0 2225.9 jit_solution(1678490124848101853)
XLA Ops:
  91.3 46.9 %scatter_fusion.1 = bf16[192,2,16,8,128]{4,3,2,1,0:T(8,128)(2,1)} fusion(bf16[192,2,16,8,128]{4,3,2,1,0:T(8,128)(2,1)} %copy.493, s32[512]{0:T(512)S(1)} %bitcast.413, bf16[512,8,128]{2,1,0:T(8,128)(2,1)S(1)} %bitcast.422), kind=kCustom, calls=%fused_computation.18 | custom fusion | bytes 3151872 | tf_op jit(solution)/shard_map/scatter | solution.py:81
  146.6 46.9 %scatter_fusion.2 = bf16[192,2,16,8,128]{4,3,2,1,0:T(8,128)(2,1)} fusion(bf16[192,2,16,8,128]{4,3,2,1,0:T(8,128)(2,1)} %copy.494, s32[512]{0:T(512)S(1)} %bitcast.414, bf16[512,8,128]{2,1,0:T(8,128)(2,1)S(1)} %bitcast.421), kind=kCustom, calls=%fused_computation.19 | custom fusion | bytes 3151872 | tf_op jit(solution)/shard_map/scatter | solution.py:82
  250.9 24.2 %scatter_fusion.4 = f32[513,8,4,128]{3,1,2,0:T(8,128)} fusion(f32[513,8,4,128]{3,1,2,0:T(8,128)} %broadcast.264.clone, s32[192]{0:T(256)S(1)} %get-tuple-element.74, f32[192,8,4,128]{3,1,2,0:T(8,128)S(1)} %copy.328), kind=kCustom, calls=%fused_computation.21 | custom fusion | flops 786432 | bytes 9437952 | tf_op jit(solution)/shard_map/scatter-add | solution.py:43
  331.8 206.1 %all_to_all.20 = f32[512,8,4,130]{3,1,2,0:T(8,128)S(1)} all-to-all(f32[512,8,4,130]{3,1,2,0:T(8,128)} %pad_maximum_fusion), channel_id=1, replica_groups=mesh['rep'=1,'kv'=8] {'kv'}, dimensions={0} | all-to-all | bytes 17039360 | tf_op jit(solution)/shard_map/all_to_all | solution.py:49
  582.3 40.3 %fusion.183.clone.2 = bf16[64,14336]{1,0:T(8,128)(2,1)} fusion(bf16[64,4096]{1,0:T(8,128)(2,1)S(1)} %fusion.153, bf16[2,4096,14336]{2,1,0:T(8,128)(2,1)} %param.28), kind=kOutput, calls=%fused_computation.187.clone.clone.clone | convolution fusion | flops 7526285312 | bytes 119799808 | tf_op jit(solution)/shard_map/dot_general | solution.py:86
  622.5 39.8 %fusion.141 = bf16[64,4096]{1,0:T(8,128)(2,1)S(1)} fusion(bf16[2,14336,4096]{2,1,0:T(8,128)(2,1)} %param.29, bf16[64,4096]{1,0:T(8,128)(2,1)S(1)} %fusion.153, bf16[64,14336]{1,0:T(8,128)(2,1)} %fusion.183.clone.2), kind=kOutput, calls=%fused_computation.167 | convolution fusion | flops 7516979200 | bytes 120324096 | tf_op jit(solution)/shard_map/dot_general | solution.py:88
  700.8 46.9 %scatter_fusion.6 = bf16[192,2,16,8,128]{4,3,2,1,0:T(8,128)(2,1)} fusion(bf16[192,2,16,8,128]{4,3,2,1,0:T(8,128)(2,1)} %scatter_fusion.1, s32[512]{0:T(512)S(1)} %bitcast.409, bf16[512,8,128]{2,1,0:T(8,128)(2,1)S(1)} %bitcast.420), kind=kCustom, calls=%fused_computation.23 | custom fusion | bytes 3151872 | tf_op jit(solution)/shard_map/scatter | solution.py:81
  747.7 46.9 %scatter_fusion.7 = bf16[192,2,16,8,128]{4,3,2,1,0:T(8,128)(2,1)} fusion(bf16[192,2,16,8,128]{4,3,2,1,0:T(8,128)(2,1)} %scatter_fusion.2, s32[512]{0:T(512)S(1)} %bitcast.410, bf16[512,8,128]{2,1,0:T(8,128)(2,1)S(1)} %bitcast.419), kind=kCustom, calls=%fused_computation.24 | custom fusion | bytes 3151872 | tf_op jit(solution)/shard_map/scatter | solution.py:82
  884.6 64.4 %all-reduce.3.cloned.1.call-done = (bf16[64,2,16,8,128]{4,3,2,1,0:T(8,128)(2,1)}, bf16[64,2,16,8,128]{4,3,2,1,0:T(8,128)(2,1)}) async-done(((bf16[64,2,16,8,128]{4,3,2,1,0:T(8,128)(2,1)}, bf16[64,2,16,8,128]{4,3,2,1,0:T(8,128)(2,1)}), (bf16[64,2,16,8,128]{4,3,2,1,0:T(8,128)(2,1)}, bf16[64,2,16,8,128]{4,3,2,1,0:T(8,128)(2,1)})) %all-reduce.3.cloned.1.call-update) | async-done | bytes 8388624 | tf_op jit(solution)/shard_map/psum | solution.py:106
  974.7 47.1 %scatter_fusion.13 = bf16[192,2,16,8,128]{4,3,2,1,0:T(8,128)(2,1)} fusion(bf16[192,2,16,8,128]{4,3,2,1,0:T(8,128)(2,1)} %scatter_fusion.12, s32[512]{0:T(512)S(1)} %bitcast.411, bf16[512,8,128]{2,1,0:T(8,128)(2,1)S(1)} %copy.359), kind=kCustom, calls=%fused_computation.32 | custom fusion | bytes 3151872 | tf_op jit(solution)/shard_map/scatter | solution.py:81
  1056.0 46.8 %scatter_fusion.16 = bf16[192,2,16,8,128]{4,3,2,1,0:T(8,128)(2,1)} fusion(bf16[192,2,16,8,128]{4,3,2,1,0:T(8,128)(2,1)} %scatter_fusion.15, s32[512]{0:T(512)S(1)} %bitcast.412, bf16[512,8,128]{2,1,0:T(8,128)(2,1)S(1)} %copy.362), kind=kCustom, calls=%fused_computation.35 | custom fusion | bytes 3151872 | tf_op jit(solution)/shard_map/scatter | solution.py:82
  1138.8 23.7 %scatter_fusion.18 = f32[513,8,4,128]{3,1,2,0:T(8,128)} fusion(f32[513,8,4,128]{3,1,2,0:T(8,128)} %broadcast.264.clone.1, s32[192]{0:T(256)S(1)} %get-tuple-element.72, f32[192,8,4,128]{3,1,2,0:T(8,128)S(1)} %copy.368), kind=kCustom, calls=%fused_computation.37 | custom fusion | flops 786432 | bytes 9437952 | tf_op jit(solution)/shard_map/scatter-add | solution.py:43
  1272.9 24.4 %scatter_fusion.9 = f32[513,8,4,128]{3,1,2,0:T(8,128)} fusion(f32[513,8,4,128]{3,1,2,0:T(8,128)} %broadcast.264.clone.3, s32[192]{0:T(256)S(1)} %copy-done.17, f32[192,8,4,128]{3,1,2,0:T(8,128)S(1)} %copy.345), kind=kCustom, calls=%fused_computation.26 | custom fusion | flops 786432 | bytes 9437952 | tf_op jit(solution)/shard_map/scatter-add | solution.py:43
  1353.9 54.0 %all-to-all-done.2 = f32[512,8,4,130]{3,1,2,0:T(8,128)} async-done(((f32[512,8,4,130]{3,1,2,0:T(8,128)}), f32[512,8,4,130]{3,1,2,0:T(8,128)}, u32[]{:S(2)}, u32[]{:S(2)}) %all-to-all-start.2) | async-done | bytes 8519712 | tf_op jit(solution)/shard_map/all_to_all | solution.py:49
  1457.0 39.0 %fusion.211.clone.5 = bf16[64,14336]{1,0:T(8,128)(2,1)S(1)} fusion(bf16[64,4096]{1,0:T(8,128)(2,1)S(1)} %fusion.150, bf16[2,4096,14336]{2,1,0:T(8,128)(2,1)} %param.28), kind=kOutput, calls=%fused_computation.203.clone.clone.clone.2 | convolution fusion | flops 7526285312 | bytes 119799808 | tf_op jit(solution)/shard_map/dot_general | solution.py:86
  1496.1 38.5 %fusion.138 = bf16[64,4096]{1,0:T(8,128)(2,1)S(1)} fusion(bf16[2,14336,4096]{2,1,0:T(8,128)(2,1)} %param.29, bf16[64,4096]{1,0:T(8,128)(2,1)S(1)} %fusion.150, bf16[64,14336]{1,0:T(8,128)(2,1)S(1)} %fusion.211.clone.5), kind=kOutput, calls=%fused_computation.166 | convolution fusion | flops 7516979200 | bytes 120324096 | tf_op jit(solution)/shard_map/dot_general | solution.py:88
  1560.0 55.4 %all-to-all-done.1 = f32[512,8,4,130]{3,1,2,0:T(8,128)} async-done(((f32[512,8,4,130]{3,1,2,0:T(8,128)}), f32[512,8,4,130]{3,1,2,0:T(8,128)}, u32[]{:S(2)}, u32[]{:S(2)}) %all-to-all-start.1) | async-done | bytes 8519712 | tf_op jit(solution)/shard_map/all_to_all | solution.py:49
  1663.8 46.8 %scatter_fusion.21 = bf16[192,2,16,8,128]{4,3,2,1,0:T(8,128)(2,1)} fusion(bf16[192,2,16,8,128]{4,3,2,1,0:T(8,128)(2,1)} %scatter_fusion.16, s32[512]{0:T(512)S(1)} %bitcast.407, bf16[512,8,128]{2,1,0:T(8,128)(2,1)S(1)} %copy.383), kind=kCustom, calls=%fused_computation.40 | custom fusion | bytes 3151872 | tf_op jit(solution)/shard_map/scatter | solution.py:82
  1720.1 46.8 %scatter_fusion.20 = bf16[192,2,16,8,128]{4,3,2,1,0:T(8,128)(2,1)} fusion(bf16[192,2,16,8,128]{4,3,2,1,0:T(8,128)(2,1)} %scatter_fusion.13, s32[512]{0:T(512)S(1)} %bitcast.408, bf16[512,8,128]{2,1,0:T(8,128)(2,1)S(1)} %copy.380), kind=kCustom, calls=%fused_computation.39 | custom fusion | bytes 3151872 | tf_op jit(solution)/shard_map/scatter | solution.py:81
  1909.5 39.0 %fusion.197.clone.5 = bf16[64,14336]{1,0:T(8,128)(2,1)S(1)} fusion(bf16[64,4096]{1,0:T(8,128)(2,1)S(1)} %copy-done.46, bf16[2,4096,14336]{2,1,0:T(8,128)(2,1)} %param.28), kind=kOutput, calls=%fused_computation.195.clone.clone.clone.2 | convolution fusion | flops 7526285312 | bytes 119799808 | tf_op jit(solution)/shard_map/dot_general | solution.py:86
  1948.5 38.4 %fusion.168 = bf16[1,64,4096]{2,1,0:T(8,128)(2,1)S(1)} fusion(bf16[2,14336,4096]{2,1,0:T(8,128)(2,1)} %param.29, bf16[64,4096]{1,0:T(8,128)(2,1)S(1)} %copy-done.46, bf16[64,14336]{1,0:T(8,128)(2,1)S(1)} %fusion.197.clone.5), kind=kOutput, calls=%fused_computation.176 | convolution fusion | flops 7516979200 | bytes 120324096 | tf_op jit(solution)/shard_map/dot_general | solution.py:88
  1986.9 106.5 %all-to-all-done.3 = f32[512,8,4,130]{3,1,2,0:T(8,128)} async-done(((f32[512,8,4,130]{3,1,2,0:T(8,128)}), f32[512,8,4,130]{3,1,2,0:T(8,128)}, u32[]{:S(2)}, u32[]{:S(2)}) %all-to-all-start.3) | async-done | bytes 8519712 | tf_op jit(solution)/shard_map/all_to_all | solution.py:49
  2138.3 40.3 %fusion.225.clone.2 = bf16[64,14336]{1,0:T(8,128)(2,1)} fusion(bf16[64,4096]{1,0:T(8,128)(2,1)S(1)} %fusion.144, bf16[2,4096,14336]{2,1,0:T(8,128)(2,1)} %param.28), kind=kOutput, calls=%fused_computation.211.clone.clone.clone | convolution fusion | flops 7526285312 | bytes 119799808 | tf_op jit(solution)/shard_map/dot_general | solution.py:86
  2178.5 39.4 %fusion.171 = bf16[1,64,4096]{2,1,0:T(8,128)(2,1)S(1)} fusion(bf16[2,14336,4096]{2,1,0:T(8,128)(2,1)} %param.29, bf16[64,4096]{1,0:T(8,128)(2,1)S(1)} %fusion.144, bf16[64,14336]{1,0:T(8,128)(2,1)} %fusion.225.clone.2), kind=kOutput, calls=%fused_computation.177 | convolution fusion | flops 7516979200 | bytes 120324096 | tf_op jit(solution)/shard_map/dot_general | solution.py:88
  (390 shorter events, 961.2 us)
Async XLA Ops:
  7.2 82.1 %all-gather.11.cloned.1.call-start = ((), (), s32[]{:S(2)}) async-start(), calls=%async_computation.5 | async-start | bytes 2359296 | tf_op jit(solution)/shard_map/all_gather | solution.py:74
  37.2 164.4 %all-gather.9.cloned.1.call-start = ((), (), s32[]{:S(2)}) async-start(), calls=%async_computation.4 | async-start | bytes 4718592 | tf_op jit(solution)/shard_map/all_gather | solution.py:73
  51.7 646.8 %all-gather.15.cloned.1.call-start = ((), (), s32[]{:S(2)}) async-start(), calls=%async_computation.7 | async-start | bytes 2359296 | tf_op jit(solution)/shard_map/all_gather | solution.py:74
  53.5 23.5 %copy-start = (s32[512]{0:T(512)S(1)}, s32[512]{0:T(512)}, u32[]{:S(2)}) copy-start(s32[512]{0:T(512)} %param.33) | copy-start | bytes 6148
  61.3 29.8 %copy-start.33 = (s32[1024]{0:T(1024)}, s32[1024]{0:T(1024)S(1)}, u32[]{:S(2)}) copy-start(s32[1024]{0:T(1024)S(1)} %reshape.531) | copy-start | bytes 12292
  61.5 29.5 %copy-start.34 = (s32[1024]{0:T(1024)}, s32[1024]{0:T(1024)S(1)}, u32[]{:S(2)}) copy-start(s32[1024]{0:T(1024)S(1)} %reshape.539) | copy-start | bytes 12292
  77.0 161.0 %copy-start.20 = (s32[1024]{0:T(1024)}, s32[1024]{0:T(1024)S(1)}, u32[]{:S(2)}) copy-start(s32[1024]{0:T(1024)S(1)} %pad_clamp_fusion.2) | copy-start | bytes 12292
  78.6 160.4 %copy-start.28 = (pred[192]{0:T(512)(128)(4,1)}, pred[192]{0:T(512)(128)(4,1)S(1)}, u32[]{:S(2)}) copy-start(pred[192]{0:T(512)(128)(4,1)S(1)} %get-tuple-element.28) | copy-start | bytes 580
  78.6 204.4 %copy-start.16 = (s32[192]{0:T(256)}, s32[192]{0:T(256)S(1)}, u32[]{:S(2)}) copy-start(s32[192]{0:T(256)S(1)} %get-tuple-element.74) | copy-start | bytes 2308
  78.8 160.7 %copy-start.12 = (pred[192,16]{1,0:T(8,128)(4,1)}, pred[192,16]{1,0:T(8,128)(4,1)S(1)}, u32[]{:S(2)}) copy-start(pred[192,16]{1,0:T(8,128)(4,1)S(1)} %copy.321) | copy-start | bytes 9220
  673.2 161.1 %all-gather.19.cloned.1.call-start = ((), (), s32[]{:S(2)}) async-start(), calls=%async_computation.9 | async-start | bytes 2359296 | tf_op jit(solution)/shard_map/all_gather | solution.py:74
  683.9 156.7 %all-gather.17.cloned.1.call-start = ((), (), s32[]{:S(2)}) async-start(), calls=%async_computation.8 | async-start | bytes 4718592 | tf_op jit(solution)/shard_map/all_gather | solution.py:73
  698.4 250.6 %all-reduce.3.cloned.1.call-start = ((), (), s32[]{:S(2)}) async-start(), calls=%async_computation.12 | async-start | bytes 16777216 | tf_op jit(solution)/shard_map/psum | solution.py:106
  815.7 408.2 %all-gather.13.cloned.1.call-start = ((), (), s32[]{:S(2)}) async-start(), calls=%async_computation.6 | async-start | bytes 4718592 | tf_op jit(solution)/shard_map/all_gather | solution.py:73
  832.3 287.4 %copy-start.22 = (s32[1024]{0:T(1024)}, s32[1024]{0:T(1024)S(1)}, u32[]{:S(2)}) copy-start(s32[1024]{0:T(1024)S(1)} %pad_clamp_fusion.1) | copy-start | bytes 12292
  834.1 292.4 %copy-start.30 = (pred[192]{0:T(512)(128)(4,1)}, pred[192]{0:T(512)(128)(4,1)S(1)}, u32[]{:S(2)}) copy-start(pred[192]{0:T(512)(128)(4,1)S(1)} %get-tuple-element.20) | copy-start | bytes 580
  834.1 336.3 %copy-start.18 = (s32[192]{0:T(256)}, s32[192]{0:T(256)S(1)}, u32[]{:S(2)}) copy-start(s32[192]{0:T(256)S(1)} %get-tuple-element.72) | copy-start | bytes 2308
  834.3 292.7 %copy-start.14 = (pred[192,16]{1,0:T(8,128)(4,1)}, pred[192,16]{1,0:T(8,128)(4,1)S(1)}, u32[]{:S(2)}) copy-start(pred[192,16]{1,0:T(8,128)(4,1)S(1)} %copy.357) | copy-start | bytes 9220
  876.4 72.6 %copy-start.32 = (s32[64]{0:T(128)S(1)}, s32[64]{0:T(128)}, u32[]{:S(2)}) copy-start(s32[64]{0:T(128)} %get-tuple-element.78) | copy-start | bytes 772
  1219.2 188.6 %all-to-all-start.2 = ((f32[512,8,4,130]{3,1,2,0:T(8,128)}), f32[512,8,4,130]{3,1,2,0:T(8,128)}, u32[]{:S(2)}, u32[]{:S(2)}) async-start(f32[512,8,4,130]{3,1,2,0:T(8,128)} %pad_maximum_fusion.2), calls=%async_computation.2 | async-start | bytes 33554432 | tf_op jit(solution)/shard_map/all_to_all | solution.py:49
  1407.9 207.5 %all-to-all-start.1 = ((f32[512,8,4,130]{3,1,2,0:T(8,128)}), f32[512,8,4,130]{3,1,2,0:T(8,128)}, u32[]{:S(2)}, u32[]{:S(2)}) async-start(f32[512,8,4,130]{3,1,2,0:T(8,128)} %pad_maximum_fusion.1), calls=%async_computation.1 | async-start | bytes 33554432 | tf_op jit(solution)/shard_map/all_to_all | solution.py:49
  1412.4 248.4 %all-gather.23.cloned.1.call-start = ((), (), s32[]{:S(2)}) async-start(), calls=%async_computation.11 | async-start | bytes 2359296 | tf_op jit(solution)/shard_map/all_gather | solution.py:74
  1545.5 229.6 %all-gather.21.cloned.1.call-start = ((), (), s32[]{:S(2)}) async-start(), calls=%async_computation.10 | async-start | bytes 4718592 | tf_op jit(solution)/shard_map/all_gather | solution.py:73
  1904.6 188.8 %all-to-all-start.3 = ((f32[512,8,4,130]{3,1,2,0:T(8,128)}), f32[512,8,4,130]{3,1,2,0:T(8,128)}, u32[]{:S(2)}, u32[]{:S(2)}) async-start(f32[512,8,4,130]{3,1,2,0:T(8,128)} %pad_maximum_fusion.3), calls=%async_computation.3 | async-start | bytes 33554432 | tf_op jit(solution)/shard_map/all_to_all | solution.py:49
  (39 other events, 420.5 us)
Sparse Core Ops, SparseCore 0:
  37.3 24.7 all-gather.10
  64.5 30.7 all-gather.8
  673.3 21.0 all-gather.14
  696.1 21.9 all-gather.18
  719.7 30.7 all-gather.16
  815.8 133.1 all-reduce.2
  950.9 30.8 all-gather.12
  1545.6 32.8 all-gather.22
  1580.9 41.8 all-gather.20
where the time goes:
time: 2250 us; the launch traced here: 2230 us
  local copies, waits for them, and re-layouts  842 us (37%)
  matrix products  521 us (23%)
  other arithmetic  346 us (15%)
  waiting for transfers between devices  281 us (12%)
  blocking collectives  206 us (9%)
    all_to_all x3, waiting for transfers between devices, merge_partials(): received = lax.all_to_all(packed, 'kv', 0, 0, tiled=True)  216 us
    all_to_all x1, blocking collectives, merge_partials(): received = lax.all_to_all(packed, 'kv', 0, 0, tiled=True)  206 us
    scatter x4, local copies, waits for them, and re-layouts, decode_layer(): k_pool.at[local_ids, layer_idx, offsets].set(kv_rows[0], mode='drop')  188 us
    scatter x4, local copies, waits for them, and re-layouts, decode_layer(): v_pool.at[local_ids, layer_idx, offsets].set(kv_rows[1], mode='drop')  187 us
    dot_general x4, matrix products, decode_layer(): jnp.dot(hidden, w_up[layer_idx], preferred_element_type=jnp.float32)  159 us
    dot_general x4, matrix products, decode_layer(): jnp.dot(act_vals, w_down[layer_idx], preferred_element_type=jnp.float32)  156 us
    scatter-add x4, other arithmetic, local_partials(): jax.ops.segment_sum(slot_out * rescale[..., None], seg_ids, num_segments=...  96 us
    unnamed x122, local copies, waits for them, and re-layouts  82.4 us
  transfers between devices with their start and end apart: 12, of which 4 were waited for; matrix products, arithmetic and copies ran while one was open for 52% of the time, Pallas kernels for 0%

commit v1 on v0

v1 whole, which is shorter than its diff:
```python
import functools

import jax
import jax.numpy as jnp
from jax import lax
from jax.experimental import pallas as pl
from jax.experimental.pallas import tpu as pltpu
from jax.sharding import PartitionSpec as P

STEPS = 2
I32 = jnp.int32


def excl_cumsum(values):
    n = values.shape[0]
    before = jnp.arange(n)[None, :] < jnp.arange(n)[:, None]
    return jnp.sum(jnp.where(before, values[None, :], 0), axis=1)


def masked_pick(mask, values):
    return jnp.sum(jnp.where(mask, values, 0), axis=-1)


def place_sequences(pref, group_size, per_dev):
    count = pref.shape[0]
    ids = jnp.arange(count)
    earlier = ids[None, :] < ids[:, None]
    rank = jnp.sum((pref[None, :] == pref[:, None]) & earlier, axis=1)
    wanted = jnp.sum(pref[None, :] == jnp.arange(group_size)[:, None], axis=1)
    free = jnp.maximum(per_dev - wanted, 0)
    free_end = excl_cumsum(free) + free
    over = rank >= per_dev
    over_rank = jnp.sum(over[None, :] & earlier, axis=1)
    spill = jnp.sum(over_rank[:, None] >= free_end[None, :], axis=1)
    dev = jnp.where(over, spill, pref)
    pos = jnp.sum((dev[None, :] == dev[:, None]) & earlier, axis=1)
    return dev.astype(I32), pos.astype(I32)


def any_spec():
    return pl.BlockSpec(memory_space=pl.ANY)


def smem_spec():
    return pl.BlockSpec(memory_space=pltpu.SMEM)


def vmem_spec():
    return pl.BlockSpec(memory_space=pltpu.VMEM)


def start(copy):
    copy.start()


def wait(copy):
    copy.wait()


def for_all(count, table, row, make, act):
    def body(e, carry):
        @pl.when(table[row, e] >= 0)
        def _():
            for copy in make(e):
                act(copy)
        return carry
    lax.fori_loop(0, count, body, 0)


def pack_kernel(layers, rows, clear, meta, k_pool, v_pool, *rest):
    outs = rest[:layers]
    stage, in_sem, out_sem = rest[-3:]
    count = stage.shape[1]

    def fetch(layer):
        def make(e):
            slot = meta[0, e]
            return (pltpu.make_async_copy(k_pool.at[slot, layer, pl.ds(0, rows)], stage.at[layer, e, 0], in_sem.at[layer]),
                    pltpu.make_async_copy(v_pool.at[slot, layer, pl.ds(0, rows)], stage.at[layer, e, 1], in_sem.at[layer]))
        return make

    for layer in range(layers):
        for_all(count, meta, 0, fetch(layer), start)
    if clear:
        def wipe(e, carry):
            @pl.when(meta[0, e] < 0)
            def _():
                for layer in range(layers):
                    stage[layer, e] = jnp.zeros(stage.shape[2:], stage.dtype)
            return carry
        lax.fori_loop(0, count, wipe, 0)
    for layer in range(layers):
        for_all(count, meta, 0, fetch(layer), wait)
        pltpu.make_async_copy(stage.at[layer], outs[layer], out_sem.at[layer]).start()
    for layer in range(layers):
        pltpu.make_async_copy(stage.at[layer], outs[layer], out_sem.at[layer]).wait()


def pack(name, k_pool, v_pool, slot_of, rows, clear, spare=()):
    layers = k_pool.shape[1]
    shape = (slot_of.shape[0], 2, rows) + k_pool.shape[3:]
    outs = [jax.ShapeDtypeStruct(shape, k_pool.dtype)] * layers + [jax.ShapeDtypeStruct(s, k_pool.dtype) for s in spare]
    return pl.pallas_call(
        functools.partial(pack_kernel, layers, rows, clear),
        out_shape=outs,
        in_specs=[smem_spec(), any_spec(), any_spec()],
        out_specs=[any_spec()] * len(outs),
        scratch_shapes=[pltpu.VMEM((layers,) + shape, k_pool.dtype), pltpu.SemaphoreType.DMA((layers,)), pltpu.SemaphoreType.DMA((layers,))],
        name=name,
    )(slot_of[None, :].astype(I32), k_pool, v_pool)


LOCAL, MOVED, NEXT, OTHER = range(4)


def attend_kernel(layer, seqs, page_len, q_per_kv, unroll, meta, q_ref, new_ref, k_pool, v_pool, moved, near, other, out_ref, k_buf, v_buf, k_sem, v_sem):
    kv_heads, head_dim = k_buf.shape[2:]
    near_rows = near.shape[2]

    def fetch(j, act):
        for page in range(2):
            kind = meta[2 * page, j]
            index = meta[2 * page + 1, j]

            def both(k_src, v_src, rows):
                dst = pl.ds(page * page_len, rows)
                act(pltpu.make_async_copy(k_src, k_buf.at[j, dst], k_sem.at[j]))
                act(pltpu.make_async_copy(v_src, v_buf.at[j, dst], v_sem.at[j]))

            @pl.when(kind == LOCAL)
            def _():
                both(k_pool.at[index, layer], v_pool.at[index, layer], page_len)

            @pl.when(kind == MOVED)
            def _():
                both(moved.at[index, 0], moved.at[index, 1], page_len)

            @pl.when(kind == NEXT)
            def _():
                both(near.at[index, 0], near.at[index, 1], near_rows)

            @pl.when(kind == OTHER)
            def _():
                both(other.at[index, 0, layer], other.at[index, 1, layer], page_len)

    def launch(j, carry):
        fetch(j, start)
        return carry
    lax.fori_loop(0, seqs, launch, 0)

    rows = STEPS * kv_heads * q_per_kv
    cols = 2 * page_len * kv_heads
    row_id = lax.broadcasted_iota(I32, (rows, cols), 0)
    col_id = lax.broadcasted_iota(I32, (rows, cols), 1)
    row_step = row_id // (kv_heads * q_per_kv)
    own_head = (col_id % kv_heads) == (row_id % (kv_heads * q_per_kv)) // q_per_kv
    lag = jnp.where(own_head, col_id // kv_heads - row_step, 1 << 20)
    v_pos = lax.broadcasted_iota(I32, (cols, head_dim), 0) // kv_heads

    def body(i, carry):
        for u in range(unroll):
            fetch(i * unroll + u, wait)
        for u in range(unroll):
            j = i * unroll + u
            length = meta[4, j]
            for step in range(STEPS):
                k_buf[j, length + step] = new_ref[j, 0, step]
                v_buf[j, length + step] = new_ref[j, 1, step]
        for u in range(unroll):
            j = i * unroll + u
            length = meta[4, j]
            keys = k_buf[j].reshape(cols, head_dim)
            vals = v_buf[j].reshape(cols, head_dim)
            vals = jnp.where(v_pos <= length + (STEPS - 1), vals.astype(jnp.float32), 0.0).astype(vals.dtype)
            query = q_ref[j].reshape(rows, head_dim)
            scores = lax.dot_general(query, keys, (((1,), (1,)), ((), ())), preferred_element_type=jnp.float32)
            scores = jnp.where(lag <= length, scores * head_dim ** -0.5, -jnp.inf)
            top = jnp.max(scores, axis=1, keepdims=True)
            probs = jnp.exp(scores - top)
            total = jnp.sum(probs, axis=1, keepdims=True)
            out = jnp.dot(probs.astype(vals.dtype), vals, preferred_element_type=jnp.float32) / total
            out_ref[j] = out.astype(out_ref.dtype).reshape(out_ref.shape[1:])
        return carry
    lax.fori_loop(0, seqs // unroll, body, 0)


def attend(layer, queries, new_rows, k_pool, v_pool, moved, near, other, meta):
    seqs = queries.shape[0]
    page_len, kv_heads, head_dim = k_pool.shape[2:]
    num_heads = queries.shape[2]
    buf = pltpu.VMEM((seqs, 2 * page_len, kv_heads, head_dim), k_pool.dtype)
    return pl.pallas_call(
        functools.partial(attend_kernel, layer, seqs, page_len, num_heads // kv_heads, 4),
        out_shape=jax.ShapeDtypeStruct(queries.shape, queries.dtype),
        in_specs=[smem_spec(), vmem_spec(), vmem_spec()] + [any_spec()] * 5,
        out_specs=vmem_spec(),
        scratch_shapes=[buf, buf, pltpu.SemaphoreType.DMA((seqs,)), pltpu.SemaphoreType.DMA((seqs,))],
        cost_estimate=pl.CostEstimate(flops=10 ** 10, bytes_accessed=10 ** 7, transcendentals=10 ** 6),
        name=f'attend_{layer}',
    )(meta, queries, new_rows, k_pool, v_pool, moved, near, other)


def finish_kernel(layers, slots, entries, mig, owner, k_in, v_in, *rest):
    del k_in, v_in
    moved = rest[:layers]
    rows = rest[layers:2 * layers]
    k_out, v_out, zeros, stage, row_stage, zero_sem, in_sem, out_sem, row_in_sem, row_sem = rest[2 * layers:]
    zeros[...] = jnp.zeros_like(zeros)

    def fetch(e):
        return [pltpu.make_async_copy(moved[layer].at[e], stage.at[layer, e], in_sem.at[e]) for layer in range(layers)]

    def put(e):
        out = []
        for layer in range(layers):
            out.append(pltpu.make_async_copy(stage.at[layer, e, 0], k_out.at[mig[1, e], layer], out_sem.at[0]))
            out.append(pltpu.make_async_copy(stage.at[layer, e, 1], v_out.at[mig[1, e], layer], out_sem.at[0]))
        return out

    def clear(e):
        return (pltpu.make_async_copy(zeros, k_out.at[mig[0, e]], zero_sem.at[0]),
                pltpu.make_async_copy(zeros, v_out.at[mig[0, e]], zero_sem.at[0]))

    def load(layer):
        return pltpu.make_async_copy(rows[layer], row_stage.at[layer], row_in_sem.at[layer])

    def fill(j):
        out = []
        for layer in range(layers):
            src = row_stage.at[layer, owner[0, j]]
            dst = pl.ds(owner[1, j], STEPS)
            out.append(pltpu.make_async_copy(src.at[0], k_out.at[j, layer, dst], row_sem.at[0]))
            out.append(pltpu.make_async_copy(src.at[1], v_out.at[j, layer, dst], row_sem.at[0]))
        return out

    for_all(entries, mig, 1, fetch, start)
    for layer in range(layers):
        load(layer).start()

    def relay(e, carry):
        @pl.when(mig[1, e] >= 0)
        def _():
            for copy in fetch(e):
                copy.wait()
            for copy in put(e):
                copy.start()
        return carry
    lax.fori_loop(0, entries, relay, 0)
    for_all(entries, mig, 0, clear, start)
    for_all(entries, mig, 1, put, wait)
    for layer in range(layers):
        load(layer).wait()
    for_all(slots, owner, 0, fill, start)
    for_all(entries, mig, 0, clear, wait)
    for_all(slots, owner, 0, fill, wait)


def finish_pools(k_pool, v_pool, moved, rows, mig, owner):
    slots, layers = k_pool.shape[:2]
    entries = mig.shape[1]
    pool = jax.ShapeDtypeStruct(k_pool.shape, k_pool.dtype)
    return pl.pallas_call(
        functools.partial(finish_kernel, layers, slots, entries),
        out_shape=[pool, pool],
        in_specs=[smem_spec(), smem_spec()] + [any_spec()] * (2 + 2 * layers),
        out_specs=[any_spec(), any_spec()],
        input_output_aliases={2: 0, 3: 1},
        scratch_shapes=[
            pltpu.VMEM(k_pool.shape[1:], k_pool.dtype),
            pltpu.VMEM((layers,) + moved[0].shape, k_pool.dtype),
            pltpu.VMEM((layers,) + rows[0].shape, k_pool.dtype),
            pltpu.SemaphoreType.DMA((1,)),
            pltpu.SemaphoreType.DMA((entries,)),
            pltpu.SemaphoreType.DMA((1,)),
            pltpu.SemaphoreType.DMA((layers,)),
            pltpu.SemaphoreType.DMA((1,)),
        ],
        name='finish_pools',
    )(mig, owner, k_pool, v_pool, *moved, *rows)


def dense(hidden, weight):
    return jnp.dot(hidden, weight, preferred_element_type=jnp.float32)


def shift_by(count, distance):
    return [(i, (i + distance) % count) for i in range(count)]


ROUND_PAGES = 8


def other_pages(k_pool, v_pool, buffer, src, slot, dst, target, wanted, me, group_size):
    entry_ids = jnp.arange(src.shape[0])
    rank = masked_pick((src[None, :] == src[:, None]) & wanted[None, :] & (entry_ids[None, :] < entry_ids[:, None]), 1)
    most = jnp.max(jnp.where(wanted, rank + 1, 0))
    seat = jnp.where(wanted, src * src.shape[0] + rank, -1)

    def body(carry):
        done, buf = carry
        seats = ((jnp.arange(group_size) * src.shape[0])[:, None] + done + jnp.arange(ROUND_PAGES)[None, :]).reshape(-1)
        hit = seat[None, :] == seats[:, None]
        seat_slot = masked_pick(hit, slot[None, :])
        seat_target = jnp.where(jnp.any(hit & (dst == me)[None, :], axis=1), masked_pick(hit, target[None, :]), buf.shape[0])
        my_slots = lax.dynamic_slice_in_dim(seat_slot, me * ROUND_PAGES, ROUND_PAGES)
        pages = jnp.stack([jnp.take(k_pool, my_slots, axis=0), jnp.take(v_pool, my_slots, axis=0)], axis=1)
        gathered = lax.all_gather(pages, 'kv', axis=0, tiled=True)
        return done + ROUND_PAGES, buf.at[seat_target].set(gathered, mode='drop')

    return lax.while_loop(lambda carry: carry[0] < most, body, (jnp.zeros((), I32), buffer))[1]


def solution(mesh):
    group_size = mesh.shape['kv']
    pool_spec = P(('rep', 'kv'))
    tok_spec = P(None, ('rep', 'kv'), None)

    def device_fn(embeds, w_query, w_key, w_value, w_out, w_up, w_down, k_pool, v_pool, new_table, seq_lens, mig_src, mig_dst):
        me = lax.axis_index('kv')
        slots, layers, page_len, kv_heads, head_dim = k_pool.shape
        per_dev, width = embeds.shape[1:]
        seq_count, page_count = new_table.shape
        num_heads = w_query.shape[2] // head_dim

        remap = new_table[:, :, None] == mig_dst
        is_moved = jnp.any(remap, axis=-1)
        move_id = masked_pick(remap, jnp.arange(mig_src.shape[0], dtype=I32))
        old_table = jnp.where(is_moved, masked_pick(remap, mig_src), new_table)
        page_src = old_table // slots
        page_slot = old_table % slots
        dev, pos = place_sequences(page_src[:, 0], group_size, per_dev)
        place = dev * per_dev + pos

        src_dev, dst_dev = mig_src // slots, mig_dst // slots
        clear_slot = jnp.where(src_dev == me, mig_src % slots, -1)
        fill_slot = jnp.where(dst_dev == me, mig_dst % slots, -1)
        mig_meta = jnp.stack([clear_slot, fill_slot]).astype(I32)
        moved = [lax.psum(pages, 'kv') for pages in pack('pack_moved', k_pool, v_pool, clear_slot, page_len, True)]

        prev = (me + group_size - 1) % group_size
        prev_seat = prev * per_dev + jnp.arange(per_dev, dtype=I32)
        from_here = (place[None, :] == prev_seat[:, None]) & ((page_src[:, 1] == me) & ~is_moved[:, 1])[None, :]
        near_slot = masked_pick(from_here, page_slot[None, :, 1] + 1) - 1
        other_shape = (per_dev * page_count, 2) + k_pool.shape[1:]
        *near_out, other = pack('pack_near', k_pool, v_pool, near_slot, page_len - 2, False, [other_shape])
        near = [lax.ppermute(pages, 'kv', shift_by(group_size, -1)) for pages in near_out]

        my_dev = lax.dynamic_slice_in_dim(dev, me * per_dev, per_dev)
        my_pos = lax.dynamic_slice_in_dim(pos, me * per_dev, per_dev)
        home = jnp.arange(seq_count, dtype=I32) // per_dev
        distance = (dev - home) % group_size
        my_distance = (my_dev - me) % group_size
        at_pos = my_pos[None, :] == jnp.arange(per_dev, dtype=I32)[:, None]

        def send_embeds(step_away, hidden):
            sel = (at_pos & (my_distance == step_away)[None, :]).astype(embeds.dtype)
            rows = jnp.einsum('pb,tbd->ptd', sel, embeds, preferred_element_type=jnp.float32).astype(embeds.dtype)
            if step_away:
                rows = lax.ppermute(rows, 'kv', shift_by(group_size, step_away))
            return hidden + rows

        hidden = jnp.zeros((per_dev, STEPS, width), embeds.dtype)
        for step_away in range(group_size):
            hidden = lax.cond(jnp.any(distance == step_away), functools.partial(send_embeds, step_away), lambda same: same, hidden)
        hidden = hidden.reshape(per_dev * STEPS, width)

        page_ids = jnp.arange(page_count, dtype=I32)[None, :]
        is_near = (page_ids == 1) & (page_src == ((dev + 1) % group_size)[:, None]) & ~is_moved
        is_local = page_src == dev[:, None]
        wanted = ~(is_local | is_moved | is_near)
        kind = jnp.where(is_local, LOCAL, jnp.where(is_moved, MOVED, jnp.where(is_near, NEXT, OTHER)))
        target = pos[:, None] * page_count + page_ids
        index = jnp.where(is_local, page_slot, jnp.where(is_moved, move_id, jnp.where(is_near, pos[:, None], target)))
        entry_dst = jnp.broadcast_to(dev[:, None], page_src.shape)
        other = other_pages(k_pool, v_pool, other, page_src.reshape(-1), page_slot.reshape(-1), entry_dst.reshape(-1), target.reshape(-1), wanted.reshape(-1), me, group_size)
        mine = place[None, :] == (me * per_dev + jnp.arange(per_dev, dtype=I32))[:, None]
        facts = jnp.stack([kind[:, 0], index[:, 0], kind[:, 1], index[:, 1], seq_lens])
        attend_meta = masked_pick(mine[None, :, :], facts[:, None, :]).astype(I32)

        writes = new_table[None, :, 1] == (me * slots + jnp.arange(slots, dtype=I32))[:, None]
        owner_place = masked_pick(writes, place[None, :] + 1) - 1
        owner_off = masked_pick(writes, seq_lens[None, :] - page_len)
        owner_meta = jnp.stack([owner_place, owner_off]).astype(I32)

        new_all = []
        for layer in range(layers):
            queries = dense(hidden, w_query[layer]).astype(jnp.bfloat16)
            new_keys = dense(hidden, w_key[layer]).astype(jnp.bfloat16)
            new_vals = dense(hidden, w_value[layer]).astype(jnp.bfloat16)
            rows = jnp.stack([new_keys, new_vals]).reshape(2, per_dev, STEPS, kv_heads, head_dim).transpose(1, 0, 2, 3, 4)
            new_all.append(lax.all_gather(rows, 'kv', axis=0, tiled=True))
            q_rows = queries.reshape(per_dev, STEPS, num_heads, head_dim)
            attn = attend(layer, q_rows, rows, k_pool, v_pool, moved[layer], near[layer], other, attend_meta).reshape(per_dev * STEPS, num_heads * head_dim)
            hidden = (hidden.astype(jnp.float32) + dense(attn, w_out[layer])).astype(jnp.bfloat16)
            up_proj = dense(hidden, w_up[layer]).astype(jnp.bfloat16)
            act = jax.nn.gelu(up_proj.astype(jnp.float32), approximate=True).astype(jnp.bfloat16)
            hidden = (hidden.astype(jnp.float32) + dense(act, w_down[layer])).astype(jnp.bfloat16)

        k_out, v_out = finish_pools(k_pool, v_pool, moved, new_all, mig_meta, owner_meta)

        hidden = hidden.reshape(per_dev, STEPS, width)

        def bring_home(step_away, total):
            rows = lax.ppermute(hidden, 'kv', shift_by(group_size, -step_away)) if step_away else hidden
            sel = (at_pos & (my_distance == step_away)[None, :]).astype(hidden.dtype)
            return total + jnp.einsum('pb,ptd->tbd', sel, rows, preferred_element_type=jnp.float32).astype(hidden.dtype)

        y_out = jnp.zeros((STEPS, per_dev, width), hidden.dtype)
        for step_away in range(group_size):
            y_out = lax.cond(jnp.any(distance == step_away), functools.partial(bring_home, step_away), lambda same: same, y_out)
        return y_out, k_out, v_out

    return jax.shard_map(device_fn, mesh=mesh, in_specs=(tok_spec, P(), P(), P(), P(), P(), P(), pool_spec, pool_spec, P('rep', None), P('rep'), P('rep'), P('rep')), out_specs=(tok_spec, pool_spec, pool_spec), check_vma=False)
```

time: 2250 us -> 564 us (0.25)
  local copies, waits for them, and re-layouts: 842 us -> 26.8 us
  other arithmetic: 346 us -> 12.5 us
  matrix products: 521 us -> 233 us
  blocking collectives: 206 us -> 0 us
  waiting for transfers between devices: 281 us -> 181 us
  Pallas kernels: 0 us -> 74.7 us
    scatter x13 -> x0, local copies, waits for them, and re-layouts: 422 us -> none  [the longest x4 188 us: decode_layer(): k_pool.at[local_ids, layer_idx, offsets].set(kv_rows[0], mode='drop')]
    dot_general x32 -> x14, matrix products: 521 us -> 233 us  [the longest x12 231 us: dense(): return jnp.dot(hidden, weight, preferred_element_type=jnp.float32)]
    all_to_all x3 -> x0, waiting for transfers between devices: 216 us -> none  [merge_partials(): received = lax.all_to_all(packed, 'kv', 0, 0, tiled=True)]
    all_to_all x1 -> x0, blocking collectives: 206 us -> none  [merge_partials(): received = lax.all_to_all(packed, 'kv', 0, 0, tiled=True)]
    ppermute x0 -> x4, waiting for transfers between devices: none -> 173 us  [the longest x1 150 us: send_embeds(): rows = lax.ppermute(rows, 'kv', shift_by(group_size, step_away))]
    scatter-add x12 -> x0, other arithmetic: 156 us -> none  [the longest x4 96 us: local_partials(): jax.ops.segment_sum(slot_out * rescale[..., None], seg_ids, num_segments=...]
    broadcast_in_dim x16 -> x3, local copies, waits for them, and re-layouts: 112 us -> 0.36 us  [the longest x1 0.17 us: masked_pick(): return jnp.sum(jnp.where(mask, values, 0), axis=-1)]
    slice x18 -> x2, local copies, waits for them, and re-layouts: 98.9 us -> 0.01 us  [the longest x1 0.01 us: device_fn(): new_table[None, :, 1]]
  transfers between devices with their start and end apart: 12 -> 7, of which waited for: 4 -> 3; matrix products, arithmetic and copies ran while one was open for 52% -> 45% of each run, Pallas kernels for 0% -> 9%
where the time goes in v1:
time: 564 us; the launch traced here: 557 us
  matrix products  233 us (41%)
  waiting for transfers between devices  181 us (32%)
  Pallas kernels  74.7 us (13%)
  local copies, waits for them, and re-layouts  26.8 us (5%)
  between operations  21.9 us (4%)
  other arithmetic  12.5 us (2%)
  starting transfers between devices  6.57 us (1%)
    dot_general x12, matrix products, dense(): return jnp.dot(hidden, weight, preferred_element_type=jnp.float32)  231 us
    ppermute x1, waiting for transfers between devices, send_embeds(): rows = lax.ppermute(rows, 'kv', shift_by(group_size, step_away))  150 us
    pallas_call x2, Pallas kernels, attend(): pl.pallas_call(functools.partial(attend_kernel, layer, seqs, page_len, nu...  48.7 us
    ppermute x1, waiting for transfers between devices, bring_home(): lax.ppermute(hidden, 'kv', shift_by(group_size, -step_away))  22.8 us
    unnamed x35, local copies, waits for them, and re-layouts  20.4 us
    pallas_call x2, Pallas kernels, pack(): pl.pallas_call(functools.partial(pack_kernel, layers, rows, clear), out_s...  13.5 us
    pallas_call x1, Pallas kernels, finish_pools(): pl.pallas_call(functools.partial(finish_kernel, layers, slots, entries),...  12.5 us
  transfers between devices with their start and end apart: 7, of which 3 were waited for; matrix products, arithmetic and copies ran while one was open for 45% of the time, Pallas kernels for 9%

profile of v1, /device:TPU:0, one launch (start us, length us, event | category | flops | bytes accessed | tf_op | source)
XLA Modules:
  0.0 557.5 jit_solution(7730370122011636368)
XLA Ops:
  8.0 11.4 %copy.213.k_pool.k_in = bf16[192,2,16,8,128]{4,3,2,1,0:T(8,128)(2,1)} copy(bf16[192,2,16,8,128]{4,3,2,1,0:T(8,128)(2,1)} %param.56) | data formatting | bytes 25165824
  20.9 4.8 copy.214.v_pool.v_in
  31.3 5.7 %pack_near.1 = (bf16[64,2,14,8,128]{4,3,2,1,0:T(8,128)(2,1)}, bf16[64,2,14,8,128]{4,3,2,1,0:T(8,128)(2,1)}, bf16[128,2,2,16,8,128]{5,4,3,2,1,0:T(8,128)(2,1)}) custom-call(s32[1,64]{1,0:T(1,128)} %add_bitcast_fusion.meta, bf16[192,2,16,8,128]{4,3,2,1,0:T(8,128)(2,1)} %copy.213.k_pool.k_in, bf16[192,2,16,8,128]{4,3,2,1,0:T(8,128)(2,1)} %copy.214.v_pool.v_in), custom_call_target="tpu_custom_call" | custom-call | tf_op jit(solution)/shard_map/pack_near/pallas_call | solution.py:103
  37.1 7.8 %pack_moved.1 = (bf16[64,2,16,8,128]{4,3,2,1,0:T(8,128)(2,1)}, bf16[64,2,16,8,128]{4,3,2,1,0:T(8,128)(2,1)}) custom-call(s32[1,64]{1,0:T(1,128)} %fusion.246.meta, bf16[192,2,16,8,128]{4,3,2,1,0:T(8,128)(2,1)} %copy.213.k_pool.k_in, bf16[192,2,16,8,128]{4,3,2,1,0:T(8,128)(2,1)} %copy.214.v_pool.v_in), custom_call_target="tpu_custom_call" | custom-call | tf_op jit(solution)/shard_map/pack_moved/pallas_call | solution.py:103
  53.7 151.0 %conditional.18 = (bf16[64,2,4096]{2,0,1:T(8,128)(2,1)S(1)}) conditional(s32[]{:T(128)} %convert_element_type.210, bf16[64,2,4096]{2,0,1:T(8,128)(2,1)S(1)} %get-tuple-element.1034, (s32[64]{0:T(128)S(1)}, pred[64,64]{0,1:T(32,128)(4,1)S(1)}, bf16[2,64,4096]{2,1,0:T(8,128)(2,1)S(1)}, bf16[64,2,4096]{2,0,1:T(8,128)(2,1)S(1)}) %tuple.333), branch_computations={%region_20.21_spmd, %region_21.22_spmd} | conditional | flops 68161600 | bytes 9449904 | solution.py:364
  54.3 149.9 %collective-permute-done.1 = bf16[64,2,4096]{2,0,1:T(8,128)(2,1)S(1)} collective-permute-done((bf16[64,2,4096]{2,0,1:T(8,128)(2,1)S(1)}, bf16[64,2,4096]{2,0,1:T(8,128)(2,1)S(1)}, u32[]{:S(2)}, u32[]{:S(2)}) %collective-permute-start.1) | collective-permute-done | bytes 1048608 | tf_op jit(solution)/shard_map/cond/branch_1_fun/ppermute | solution.py:359
  208.0 6.6 %conditional.23 = (bf16[128,4096]{1,0:T(8,128)(2,1)}, bf16[128,4096]{1,0:T(8,128)(2,1)S(1)}, f32[128,4096]{1,0:T(8,128)}) conditional(s32[]{:T(128)} %convert_element_type.205, (bf16[64,2,4096]{2,0,1:T(8,128)(2,1)S(1)}) %conditional.22, (s32[64]{0:T(128)S(1)}, pred[64,64]{0,1:T(32,128)(4,1)S(1)}, bf16[2,64,4096]{2,1,0:T(8,128)(2,1)S(1)}, ...), branch_computations={%region_30.31_spmd, %region_31.32_spmd} | conditional | flops 68685888 | bytes 18887104 | solution.py:364
  214.5 4.7 fusion.222
  219.3 4.7 fusion.219
  225.5 13.0 %fusion.198 = bf16[16,8,32,128]{3,1,2,0:T(8,128)(2,1)S(1)} fusion(bf16[128,4096]{1,0:T(8,128)(2,1)S(1)} %get-tuple-element.392, bf16[2,4096,4096]{2,1,0:T(8,128)(2,1)} %param.50), kind=kOutput, calls=%fused_computation.199 | convolution fusion | flops 4295491584 | bytes 35651584 | tf_op jit(solution)/shard_map/dot_general | solution.py:283
  242.1 7.9 %all-reduce.3.cloned.1.call-done = (bf16[64,2,16,8,128]{4,3,2,1,0:T(8,128)(2,1)}, bf16[64,2,16,8,128]{4,3,2,1,0:T(8,128)(2,1)}) async-done(((bf16[64,2,16,8,128]{4,3,2,1,0:T(8,128)(2,1)}, bf16[64,2,16,8,128]{4,3,2,1,0:T(8,128)(2,1)}), (bf16[64,2,16,8,128]{4,3,2,1,0:T(8,128)(2,1)}, bf16[64,2,16,8,128]{4,3,2,1,0:T(8,128)(2,1)})) %all-reduce.3.cloned.1.call-update) | async-done | bytes 8388624 | tf_op jit(solution)/shard_map/psum | solution.py:338
  250.0 24.3 %attend_0.1 = bf16[64,2,32,128]{3,2,1,0:T(8,128)(2,1)} custom-call(s32[5,64]{1,0:T(8,128)} %select_reduce_fusion.1.meta, bf16[64,2,32,128]{3,2,1,0:T(8,128)(2,1)} %bitcast.311, bf16[64,2,2,8,128]{4,3,2,1,0:T(8,128)(2,1)} %maximum_bitcast_fusion.new_ref, bf16[192,2,16,8,128]{4,3,2,1,0:T(8,128)(2,1)} %get-tuple-element.1053, ...), custom_call_target="tpu_custom_call" | custom-call | flops 10000000000 | bytes 10000000 | tf_op jit(solution)/shard_map/attend_0/pallas_call | solution.py:192
  274.2 14.0 %fusion.177 = bf16[128,4096]{1,0:T(8,128)(2,1)S(1)} fusion(f32[128,4096]{1,0:T(8,128)} %get-tuple-element.401, bf16[2,4096,4096]{2,1,0:T(8,128)(2,1)} %param.53, bf16[16,8,32,128]{3,2,1,0:T(8,128)(2,1)} %bitcast.318), kind=kOutput, calls=%fused_computation.184 | convolution fusion | flops 4296015872 | bytes 37748736 | tf_op jit(solution)/shard_map/dot_general | solution.py:283
  288.2 40.7 %fusion.129.clone.9 = bf16[128,14336]{1,0:T(8,128)(2,1)} fusion(bf16[128,4096]{1,0:T(8,128)(2,1)S(1)} %fusion.177, bf16[2,4096,14336]{2,1,0:T(8,128)(2,1)} %param.54), kind=kOutput, calls=%fused_computation.168.clone.clone.clone.clone.clone.clone.clone.2 | convolution fusion | flops 15052570624 | bytes 122159104 | tf_op jit(solution)/shard_map/dot_general | solution.py:283
  329.0 39.0 %fusion.169 = bf16[128,4096]{1,0:T(8,128)(2,1)S(1)} fusion(bf16[2,14336,4096]{2,1,0:T(8,128)(2,1)} %param.55, bf16[128,4096]{1,0:T(8,128)(2,1)S(1)} %fusion.177, bf16[128,14336]{1,0:T(8,128)(2,1)} %fusion.129.clone.9), kind=kOutput, calls=%fused_computation.182 | convolution fusion | flops 15033958400 | bytes 123207680 | tf_op jit(solution)/shard_map/dot_general | solution.py:283
  372.6 4.6 fusion.213
  377.3 12.9 %fusion.195 = bf16[16,8,32,128]{3,1,2,0:T(8,128)(2,1)S(1)} fusion(bf16[128,4096]{1,0:T(8,128)(2,1)S(1)} %fusion.169, bf16[2,4096,4096]{2,1,0:T(8,128)(2,1)} %param.50), kind=kOutput, calls=%fused_computation.198 | convolution fusion | flops 4295491584 | bytes 35651584 | tf_op jit(solution)/shard_map/dot_general | solution.py:283
  392.4 24.4 %attend_1.1 = bf16[64,2,32,128]{3,2,1,0:T(8,128)(2,1)} custom-call(s32[5,64]{1,0:T(8,128)} %select_reduce_fusion.1.meta, bf16[64,2,32,128]{3,2,1,0:T(8,128)(2,1)} %bitcast.312, bf16[64,2,2,8,128]{4,3,2,1,0:T(8,128)(2,1)} %maximum_bitcast_fusion.1.new_ref, bf16[192,2,16,8,128]{4,3,2,1,0:T(8,128)(2,1)} %get-tuple-element.1053, ...), custom_call_target="tpu_custom_call" | custom-call | flops 10000000000 | bytes 10000000 | tf_op jit(solution)/shard_map/attend_1/pallas_call | solution.py:192
  416.8 13.5 %fusion.174 = bf16[128,4096]{1,0:T(8,128)(2,1)S(1)} fusion(bf16[2,4096,4096]{2,1,0:T(8,128)(2,1)} %param.53, bf16[128,4096]{1,0:T(8,128)(2,1)S(1)} %fusion.169, bf16[16,8,32,128]{3,2,1,0:T(8,128)(2,1)} %bitcast.317), kind=kOutput, calls=%fused_computation.183 | convolution fusion | flops 4296540160 | bytes 36700160 | tf_op jit(solution)/shard_map/dot_general | solution.py:283
  430.2 40.9 %fusion.143.clone.9 = bf16[128,14336]{1,0:T(8,128)(2,1)} fusion(bf16[128,4096]{1,0:T(8,128)(2,1)S(1)} %fusion.174, bf16[2,4096,14336]{2,1,0:T(8,128)(2,1)} %param.54), kind=kOutput, calls=%fused_computation.176.clone.clone.clone.clone.clone.clone.clone.2 | convolution fusion | flops 15052570624 | bytes 122159104 | tf_op jit(solution)/shard_map/dot_general | solution.py:283
  471.1 38.8 %fusion.164 = bf16[128,4096]{1,0:T(8,128)(2,1)S(1)} fusion(bf16[2,14336,4096]{2,1,0:T(8,128)(2,1)} %param.55, bf16[128,4096]{1,0:T(8,128)(2,1)S(1)} %fusion.174, bf16[128,14336]{1,0:T(8,128)(2,1)} %fusion.143.clone.9), kind=kOutput, calls=%fused_computation.181 | convolution fusion | flops 15033958400 | bytes 123207680 | tf_op jit(solution)/shard_map/dot_general | solution.py:283
  510.9 25.7 %conditional.26 = (bf16[2,64,4096]{2,1,0:T(8,128)(2,1)S(1)}) conditional(s32[]{:T(128)} %convert_element_type.210, bf16[2,64,4096]{2,1,0:T(8,128)(2,1)S(1)} %get-tuple-element.1041, (s32[64]{0:T(128)S(1)}, pred[64,64]{0,1:T(32,128)(4,1)S(1)}, bf16[64,2,4096]{2,1,0:T(2,128)(2,1)S(1)}, bf16[2,64,4096]{2,1,0:T(8,128)(2,1)S(1)}) %tuple.351), branch_computations={%region_49.51_spmd, %region_50.52_spmd} | conditional | flops 68161600 | bytes 9441712 | solution.py:410
  513.0 22.8 %collective-permute-done.8 = bf16[64,2,4096]{2,0,1:T(8,128)(2,1)S(1)} collective-permute-done((bf16[64,2,4096]{2,0,1:T(8,128)(2,1)S(1)}, bf16[64,2,4096]{2,0,1:T(8,128)(2,1)S(1)}, u32[]{:S(2)}, u32[]{:S(2)}) %collective-permute-start.8) | collective-permute-done | bytes 1048608 | tf_op jit(solution)/shard_map/cond/branch_1_fun/ppermute | solution.py:404
  536.9 12.5 %finish_pools.1 = (bf16[192,2,16,8,128]{4,3,2,1,0:T(8,128)(2,1)}, bf16[192,2,16,8,128]{4,3,2,1,0:T(8,128)(2,1)}) custom-call(s32[2,64]{1,0:T(2,128)} %pad_add_fusion.1.mig, s32[2,192]{1,0:T(2,128)} %pad_add_fusion.owner, bf16[192,2,16,8,128]{4,3,2,1,0:T(8,128)(2,1)} %get-tuple-element.1053, ...), custom_call_target="tpu_custom_call", output_to_operand_aliasing={{0}: (2, {}), {1}: (3, {})} | custom-call | tf_op jit(solution)/shard_map/finish_pools/pallas_call | solution.py:262
  (129 shorter events, 37.3 us)
Async XLA Ops:
  8.0 12.9 %copy-start.2 = (bf16[192,2,16,8,128]{4,3,2,1,0:T(8,128)(2,1)S(1)}, bf16[192,2,16,8,128]{4,3,2,1,0:T(8,128)(2,1)}, u32[]{:S(2)}) copy-start(bf16[192,2,16,8,128]{4,3,2,1,0:T(8,128)(2,1)} %param.57) | copy-start | bytes 37748740
  20.9 4.8 copy-start.6
  20.9 4.8 copy-start.9
  20.9 4.9 copy-start.12
  30.4 6.6 %copy-start.5 = (s32[512,2]{1,0:T(8,128)}, s32[512,2]{1,0:T(8,128)S(1)}, u32[]{:S(2)}) copy-start(s32[512,2]{1,0:T(8,128)S(1)} %copy.115) | copy-start | bytes 12292
  45.5 6.8 %copy-start = (bf16[2,64,4096]{2,1,0:T(8,128)(2,1)S(1)}, bf16[2,64,4096]{2,1,0:T(8,128)(2,1)}, u32[]{:S(2)}) copy-start(bf16[2,64,4096]{2,1,0:T(8,128)(2,1)} %param.49) | copy-start | bytes 3145732
  45.5 204.5 %all-reduce.3.cloned.1.call-start = ((), (), s32[]{:S(2)}) async-start(), calls=%async_computation.2 | async-start | bytes 16777216 | tf_op jit(solution)/shard_map/psum | solution.py:338
  46.1 490.8 %all-gather.4.cloned.1.call-start = ((), (), s32[]{:S(2)}) async-start(), calls=%async_computation | async-start | bytes 4718592 | tf_op jit(solution)/shard_map/all_gather | solution.py:391
  46.1 195.9 %collective-permute-start.14 = (bf16[64,2,14,8,128]{4,3,2,1,0:T(8,128)(2,1)}, bf16[64,2,14,8,128]{4,3,2,1,0:T(8,128)(2,1)}, u32[]{:S(2)}, u32[]{:S(2)}) collective-permute-start(bf16[64,2,14,8,128]{4,3,2,1,0:T(8,128)(2,1)} %get-tuple-element.394), channel_id=1, source_target_pairs={{0,7},{1,0},{2,1},{3,2},{4,3},{5,4},{6,5},{7,6}} | collective-permute-start | bytes 11010056 | tf_op jit(solution)/shard_map/ppermute | solution.py:346
  49.5 342.9 %collective-permute-start.15 = (bf16[64,2,14,8,128]{4,3,2,1,0:T(8,128)(2,1)}, bf16[64,2,14,8,128]{4,3,2,1,0:T(8,128)(2,1)}, u32[]{:S(2)}, u32[]{:S(2)}) collective-permute-start(bf16[64,2,14,8,128]{4,3,2,1,0:T(8,128)(2,1)} %get-tuple-element.398), channel_id=1, source_target_pairs={{0,7},{1,0},{2,1},{3,2},{4,3},{5,4},{6,5},{7,6}} | collective-permute-start | bytes 11010056 | tf_op jit(solution)/shard_map/ppermute | solution.py:346
  52.2 155.8 %copy-start.10 = (s32[64]{0:T(128)}, s32[64]{0:T(128)S(1)}, u32[]{:S(2)}) copy-start(s32[64]{0:T(128)S(1)} %and_select_fusion.7) | copy-start | bytes 772
  52.3 155.7 %copy-start.3 = (pred[64,64]{0,1:T(32,128)(4,1)}, pred[64,64]{0,1:T(32,128)(4,1)S(1)}, u32[]{:S(2)}) copy-start(pred[64,64]{0,1:T(32,128)(4,1)S(1)} %iota_compare_fusion.2) | copy-start | bytes 12292
  54.3 149.9 %collective-permute-start.1 = (bf16[64,2,4096]{2,0,1:T(8,128)(2,1)S(1)}, bf16[64,2,4096]{2,0,1:T(8,128)(2,1)S(1)}, u32[]{:S(2)}, u32[]{:S(2)}) collective-permute-start(bf16[64,2,4096]{2,0,1:T(8,128)(2,1)S(1)} %convolution_convert_fusion.2), channel_id=1, source_target_pairs={{0,2},{1,3},{2,4},{3,5},{4,6},{5,7},{6,0},{7,1}} | collective-permute-start | bytes 3145736 | tf_op jit(solution)/shard_map/cond/branch_1_fun/ppermute | solution.py:359
  225.0 311.9 %all-gather.6.cloned.1.call-start = ((), (), s32[]{:S(2)}) async-start(), calls=%async_computation.1 | async-start | bytes 4718592 | tf_op jit(solution)/shard_map/all_gather | solution.py:391
  225.5 14.2 %copy-start.7 = (s32[512]{0:T(512)S(1)}, s32[512]{0:T(512)}, u32[]{:S(2)}) copy-start(s32[512]{0:T(512)} %param.59) | copy-start | bytes 6148
  225.5 14.3 %copy-start.8 = (s32[1,64]{1,0:T(1,128)S(1)}, s32[1,64]{1,0:T(1,128)}, u32[]{:S(2)}) copy-start(s32[1,64]{1,0:T(1,128)} %fusion.246.meta) | copy-start | bytes 772
  471.1 39.5 %copy-start.4 = (pred[64,64]{0,1:T(32,128)(4,1)S(1)}, pred[64,64]{0,1:T(32,128)(4,1)}, u32[]{:S(2)}) copy-start(pred[64,64]{0,1:T(32,128)(4,1)} %copy-done.3) | copy-start | bytes 12292
  471.1 39.6 %copy-start.11 = (s32[64]{0:T(128)S(1)}, s32[64]{0:T(128)}, u32[]{:S(2)}) copy-start(s32[64]{0:T(128)} %copy-done.10) | copy-start | bytes 772
  511.5 24.4 %collective-permute-start.8 = (bf16[64,2,4096]{2,0,1:T(8,128)(2,1)S(1)}, bf16[64,2,4096]{2,0,1:T(8,128)(2,1)S(1)}, u32[]{:S(2)}, u32[]{:S(2)}) collective-permute-start(bf16[64,2,4096]{2,0,1:T(8,128)(2,1)S(1)} %copy.118), channel_id=1, source_target_pairs={{0,6},{1,7},{2,0},{3,1},{4,2},{5,3},{6,4},{7,5}} | collective-permute-start | bytes 3145736 | tf_op jit(solution)/shard_map/cond/branch_1_fun/ppermute | solution.py:404
  536.9 12.6 %copy-start.1 = (bf16[2,64,4096]{2,1,0:T(8,128)(2,1)}, bf16[2,64,4096]{2,1,0:T(8,128)(2,1)S(1)}, u32[]{:S(2)}) copy-start(bf16[2,64,4096]{2,1,0:T(8,128)(2,1)S(1)} %get-tuple-element.1047) | copy-start | bytes 3145732
Sparse Core Ops, SparseCore 1:
  49.7 200.2 all-reduce.2
  251.7 30.9 all-gather.3
  392.4 30.9 all-gather.5
